TPU v7x, 32 devices: a whole 2x2x4 slice. The times are simulated.
32 devices in a mesh: dp: 16 (over z, y, core), tensor: 2 (over x).
Axes of the slice: x: 2, y: 2, z: 4, core: 2. Of those that a mesh axis runs over, the one named last changes fastest.
Arguments:
- activations: bfloat16 [4096, 27648], P('dp', 'tensor'), may hold values from -6 to 6
- output_gradient: bfloat16 [4096, 5120], P('dp', 'tensor'), may hold values from -6 to 6
- adapter_a: bfloat16 [2, 13824, 128], P('tensor', 'dp'), may hold values from -0.0390625 to 0.0390625
- adapter_b: bfloat16 [128, 5120], P(None, 'tensor'), may hold values from -0.078125 to 0.078125
- log_ratio: float32 [4096], P('dp'), may hold values from -1.5 to 1.5
- lengths: int32 [1, 16], replicated, may hold values from 1 to 256, as said below
- rewards: int32 [1, 16], replicated, may hold values from 0 to 10
Outputs:
- grad_a: float32 [2, 13824, 128], P('tensor', 'dp')
- adapter_b_gradient: float32 [128, 5120], P(None, 'tensor')
- loss: float32 [], replicated
Inputs may be any that keep to these rules, and one draw needn't show every extreme that they name: `lengths`: in every group some rollout has length 256.
All inputs are finite; a program needn't handle non-finite values.
Results may differ from a plain program's by a relative error of at most 0.0067.
Values may be sent and summed in bfloat16 or wider, within the bound.
A program may use at most 64 MiB of HBM per device.

v0:
```python
import jax
import jax.numpy as jnp
from jax import lax
from jax.sharding import PartitionSpec as P

clip_eps = 0.2
adapter_scale_factor = 2.0


def token_terms(length_row, reward_row, log_ratio, offset):
    reward = reward_row.astype(jnp.float32)
    center = jnp.mean(reward)
    spread = jnp.mean((reward - center) * (reward - center))
    advantage = (reward - center) / jnp.sqrt(spread + 1.0)
    ends = jnp.cumsum(length_row)
    starts = ends - length_row
    slots = jnp.arange(log_ratio.shape[0], dtype=jnp.int32) + offset
    member = ((slots[None, :] >= starts[:, None]) & (slots[None, :] < ends[:, None])).astype(
        jnp.float32
    )
    live = jnp.sum(member, axis=0)
    token_adv = jnp.sum(member * advantage[:, None], axis=0)
    ratio = jnp.exp(log_ratio)
    unclipped = ratio * token_adv
    clipped = jnp.clip(ratio, 1.0 - clip_eps, 1.0 + clip_eps) * token_adv
    token_loss = -jnp.minimum(unclipped, clipped)
    slope = jnp.where(unclipped <= clipped, -unclipped, jnp.zeros_like(unclipped))
    return (live * slope, jnp.sum(live * token_loss), jnp.sum(live))


def local(activations, output_gradient, adapter_a, adapter_b, log_ratio, lengths, rewards):
    tokens = activations.shape[0]
    groups = lengths.shape[0]
    per_group = lax.axis_size("dp") // groups
    position = lax.axis_index("dp")
    group_id = position // per_group
    offset = position % per_group * tokens
    length_row = lax.dynamic_index_in_dim(lengths, group_id, 0, keepdims=False)
    reward_row = lax.dynamic_index_in_dim(rewards, group_id, 0, keepdims=False)
    token_coefficient, loss_local, live_count = token_terms(
        length_row, reward_row, log_ratio, offset
    )
    columns = activations
    partial_low = jnp.dot(
        columns,
        lax.all_gather(adapter_a, "dp", axis=1, tiled=True)[0],
        preferred_element_type=jnp.float32,
    )
    partial_back = lax.dot_general(
        output_gradient, adapter_b, (((1,), (1,)), ((), ())), preferred_element_type=jnp.float32
    )
    low_rank, backward_projection = lax.psum((partial_low, partial_back), "tensor")
    error_rows = (adapter_scale_factor * token_coefficient[:, None] * backward_projection).astype(
        jnp.bfloat16
    )
    weighted_error = token_coefficient[:, None] * low_rank
    local_adapter_b_gradient = adapter_scale_factor * jnp.einsum(
        "tr,td->rd",
        weighted_error,
        output_gradient.astype(jnp.float32),
        precision=lax.Precision.HIGHEST,
    )
    columns = activations
    grad_a = lax.psum_scatter(
        lax.dot_general(
            columns, error_rows, (((0,), (0,)), ((), ())), preferred_element_type=jnp.float32
        ),
        "dp",
        scatter_dimension=0,
        tiled=True,
    )
    grad_b_sum, loss_sum, live_sum = lax.psum(
        (local_adapter_b_gradient, loss_local, live_count), "dp"
    )
    factor = groups / live_sum
    return ((factor * grad_a)[None], factor * grad_b_sum, factor * loss_sum)


def solution(mesh):
    in_specs = (
        P("dp", "tensor"),
        P("dp", "tensor"),
        P("tensor", "dp", None),
        P(None, "tensor"),
        P("dp"),
        P(),
        P(),
    )
    out_specs = (P("tensor", "dp", None), P(None, "tensor"), P())
    return jax.shard_map(local, mesh=mesh, in_specs=in_specs, out_specs=out_specs, check_vma=False)
```

profile of v0, /device:TPU:0, one launch (start us, length us, event | category | flops | bytes accessed | tf_op | source)
XLA Modules:
  0.0 290.5 jit_solution(11864515134774246795)
XLA Ops:
  7.2 0.0 copy-start
  7.2 0.0 all-gather.2.cloned.1.call-start
  7.2 0.7 all-gather.2.cloned.1.call-update
  7.9 0.0 all-reduce.7.cloned.1.call-start
  8.0 1.3 convert_reduce_fusion.2
  9.9 1.3 multiply_reduce_fusion.1
  11.8 0.7 copy.16
  12.6 0.1 reduce.3
  12.7 0.7 divide_bitcast_fusion
  13.4 0.7 bitcast_subtract_fusion
  14.1 0.0 copy-done
  14.1 2.2 fusion.7
  16.3 0.0 copy-start.2
  16.3 43.8 %all-gather.2.cloned.1.call-done = bf16[1,13824,128]{2,1,0:T(8,128)(2,1)} async-done(((bf16[1,864,128]{2,1,0:T(8,128)(2,1)}), bf16[1,13824,128]{2,1,0:T(8,128)(2,1)}) %all-gather.2.cloned.1.call-update) | async-done | bytes 3538960 | tf_op jit(solution)/shard_map/all_gather | solution.py:46
  60.2 6.7 %fusion = f32[256,128]{1,0:T(8,128)} fusion(bf16[256,13824]{1,0:T(8,128)(2,1)} %param.7, bf16[1,13824,128]{2,1,0:T(8,128)(2,1)} %all-gather.2.cloned.1.call-done), kind=kOutput, calls=%fused_computation.2 | convolution fusion | flops 905969664 | bytes 10747904 | tf_op jit(solution)/shard_map/dot_general | solution.py:44
  66.8 0.0 all-reduce.7.cloned.1.call-update
  66.9 0.0 all-reduce.5.cloned.1.call-start
  66.9 0.7 convert_reduce_fusion.1
  67.6 0.0 copy-done.2
  67.6 0.6 broadcast_multiply_fusion.1
  68.2 20.8 %all-reduce.7.cloned.1.call-done = (f32[256,128]{1,0:T(8,128)}, f32[256,128]{1,0:T(8,128)}) async-done(((f32[256,128]{1,0:T(8,128)}, f32[256,128]{1,0:T(8,128)}), (f32[256,128]{1,0:T(8,128)}, f32[256,128]{1,0:T(8,128)})) %all-reduce.7.cloned.1.call-update) | async-done | bytes 262160 | tf_op jit(solution)/shard_map/psum | solution.py:52
  88.9 2.7 convolution_multiply_fusion
  91.7 0.0 copy-start.1
  91.7 0.0 all-reduce.5.cloned.1.call-update
  91.7 0.0 reduce-scatter.4.cloned.1.call-start
  91.8 0.8 copy-done.1
  92.6 7.2 %convolution_bitcast_fusion = f32[13824,128]{0,1:T(8,128)} fusion(bf16[256,13824]{1,0:T(8,128)(2,1)} %param.7, f32[256,128]{1,0:T(8,128)S(1)} %copy-done.1, f32[256]{0:T(256)S(1)} %get-tuple-element.22), kind=kOutput, calls=%fused_computation | convolution fusion | flops 906035200 | bytes 14287872 | tf_op jit(solution)/shard_map/dot_general | solution.py:65
  99.8 8.4 %copy.18 = f32[13824,128]{1,0:T(8,128)} copy(f32[13824,128]{0,1:T(8,128)} %convolution_bitcast_fusion) | data formatting | bytes 14155776
  108.2 0.0 reduce-scatter.4.cloned.1.call-update
  108.2 33.6 %all-reduce = (f32[]{:T(128)}, f32[]{:T(128)}) all-reduce(f32[]{:T(128)} %get-tuple-element.15, f32[]{:T(128)} %get-tuple-element.24), channel_id=1, replica_groups=mesh['dp'=16,'tensor'=2] {'dp'}, use_global_device_ids=true, to_apply=%region_2.3 | all-reduce | flops 2 | bytes 16 | tf_op jit(solution)/shard_map/psum | solution.py:72
  143.1 44.0 %all-reduce.5.cloned.1.call-done = f32[128,2560]{1,0:T(8,128)} async-done(((f32[128,2560]{1,0:T(8,128)}), f32[128,2560]{1,0:T(8,128)}) %all-reduce.5.cloned.1.call-update) | async-done | bytes 1310736 | tf_op jit(solution)/shard_map/psum | solution.py:72
  187.1 2.5 broadcast_multiply_fusion
  189.6 91.1 %reduce-scatter.4.cloned.1.call-done = f32[864,128]{1,0:T(8,128)} async-done(((f32[13824,128]{1,0:T(8,128)}), f32[864,128]{1,0:T(8,128)}) %reduce-scatter.4.cloned.1.call-update) | async-done | bytes 442384
  280.6 1.2 copy.19
  281.9 1.0 copy.17
  (3 shorter events, 0.1 us)
Async XLA Ops:
  7.2 6.9 %copy-start = (bf16[256,2560]{1,0:T(8,128)(2,1)S(1)}, bf16[256,2560]{1,0:T(8,128)(2,1)}, u32[]{:S(2)}) copy-start(bf16[256,2560]{1,0:T(8,128)(2,1)} %param.8) | copy-start | bytes 3932164
  7.2 53.0 %all-gather.2.cloned.1.call-start = ((), (), s32[]{:S(2)}) async-start(), calls=%async_computation.1 | async-start | bytes 3760128 | tf_op jit(solution)/shard_map/all_gather | solution.py:46
  7.9 81.0 %all-reduce.7.cloned.1.call-start = ((), (), s32[]{:S(2)}) async-start(), calls=%async_computation.4 | async-start | bytes 524288 | tf_op jit(solution)/shard_map/psum | solution.py:52
  16.3 51.3 %copy-start.2 = (f32[256]{0:T(256)S(1)}, f32[256]{0:T(256)}, u32[]{:S(2)}) copy-start(f32[256]{0:T(256)} %param.11) | copy-start | bytes 3076
  66.9 120.3 %all-reduce.5.cloned.1.call-start = ((), (), s32[]{:S(2)}) async-start(), calls=%async_computation.2 | async-start | bytes 2621440 | tf_op jit(solution)/shard_map/psum | solution.py:72
  91.7 0.9 copy-start.1
  91.7 188.9 %reduce-scatter.4.cloned.1.call-start = ((), (), s32[]{:S(2)}) async-start(), calls=%async_computation.3 | async-start | bytes 7520256
Sparse Core Ops, SparseCore 0:
  10.3 49.8 all-gather.1
  67.0 21.9 all-reduce.6
  93.0 94.0 all-reduce.4
  191.0 89.6 reduce-scatter.3
where the time goes:
time: 291 us
  waiting for transfers between devices  200 us (69%)
  blocking collectives  33.6 us (12%)
  matrix products  18.8 us (6%)
  between operations  17.6 us (6%)
  local copies, waits for them, and re-layouts  12.2 us (4%)
  other arithmetic  7.82 us (3%)
    unnamed x5, waiting for transfers between devices  91.8 us
    psum x1, waiting for transfers between devices, local(): lax.psum((local_adapter_b_gradient, loss_local, live_count), 'dp')  44 us
    all_gather x1, waiting for transfers between devices, local(): lax.all_gather(adapter_a, 'dp', axis=1, tiled=True)[0]  43.8 us
    psum x1, blocking collectives, local(): lax.psum((local_adapter_b_gradient, loss_local, live_count), 'dp')  33.6 us
    psum x1, waiting for transfers between devices, local(): lax.psum((partial_low, partial_back), 'tensor')  20.8 us
    unnamed x9, local copies, waits for them, and re-layouts  11.4 us
    dot_general x1, matrix products, local(): lax.dot_general(columns, error_rows, (((0,), (0,)), ((), ())), preferred_...  7.15 us
    dot_general x1, matrix products, local(): jnp.dot(columns, lax.all_gather(adapter_a, 'dp', axis=1, tiled=True)[0],...  6.66 us
  transfers between devices with their start and end apart: 4, of which 4 were waited for; matrix products, arithmetic and copies ran while one was open for 9% of the time, Pallas kernels for 0%

commit v1 on v0

--- a/solution.py
+++ b/solution.py
@@ -1,6 +1,10 @@
+import functools
+
 import jax
 import jax.numpy as jnp
 from jax import lax
+from jax.experimental import pallas as pl
+from jax.experimental.pallas import tpu as pltpu
 from jax.sharding import PartitionSpec as P
 
 clip_eps = 0.2
@@ -28,7 +32,7 @@
     return (live * slope, jnp.sum(live * token_loss), jnp.sum(live))
 
 
-def local(activations, output_gradient, adapter_a, adapter_b, log_ratio, lengths, rewards):
+def plain_local(activations, output_gradient, adapter_a, adapter_b, log_ratio, lengths, rewards):
     tokens = activations.shape[0]
     groups = lengths.shape[0]
     per_group = lax.axis_size("dp") // groups
@@ -76,6 +80,373 @@
     return ((factor * grad_a)[None], factor * grad_b_sum, factor * loss_sum)
 
 
+MESH = pl.DeviceIdType.MESH
+f32, bf16 = jnp.float32, jnp.bfloat16
+
+
+def tile_of(total, most):
+    return max(k for k in range(128, most + 1, 128) if total % k == 0)
+
+
+def fused_kernel(
+    n, groups, rollouts,
+    act_hbm, grad_hbm, a_hbm, b_hbm, ratio_ref, len_ref, rew_ref,
+    out_a, out_b, out_loss,
+    act, grad, b_mat, a_all, part, rs1, rs2, rs3, xs, xr, coef, err,
+    gb, gbs, gb1, gb2s, gb2, gb3s, gb3, fin, ls, l1, l2, lz,
+    loc, ag_s, ag_r, rs1_s, rs1_r, rs2_s, rs2_r, rs3_s, rs3_r, x_s, x_r,
+    g_s, g_r, gz_s, gz_r, fz_s, fz_r, l_s, l_r, lz_s, lz_r,
+):
+    depth = n // 4
+    p = lax.axis_index("dp")
+    t = lax.axis_index("tensor")
+    c, y, z = p % 2, (p // 2) % 2, p // 4
+    tokens, ff = act.shape
+    rows, rank = a_hbm.shape
+
+    def at(zz, yy, cc):
+        return (zz * 2 + yy) * 2 + cc
+
+    def turn(k):
+        return lax.rem(z + (k + depth), depth)
+
+    def block(ref, q):
+        return ref.at[pl.ds(pl.multiple_of(q * rows, 16), rows)]
+
+    def remote(s, d, ss, rs, dev, tensor=None):
+        return pltpu.make_async_remote_copy(
+            src_ref=s, dst_ref=d, send_sem=ss, recv_sem=rs,
+            device_id=(dev, t if tensor is None else tensor), device_id_type=MESH,
+        )
+
+    core, side = at(z, y, 1 - c), at(z, 1 - y, c)
+    zs = [turn(k) for k in range(depth)]
+    peer = [at(zs[k], y, c) for k in range(depth)]
+
+    load_a = pltpu.make_async_copy(a_hbm, block(a_all, p), loc.at[0])
+    load_g = pltpu.make_async_copy(grad_hbm, grad, loc.at[1])
+    load_b = pltpu.make_async_copy(b_hbm, b_mat, loc.at[2])
+    load_x = pltpu.make_async_copy(act_hbm, act, loc.at[3])
+    for copy in (load_a, load_g, load_b, load_x):
+        copy.start()
+
+    barrier = pltpu.get_barrier_semaphore()
+    for dev in [core, side] + peer[1:]:
+        pl.semaphore_signal(barrier, inc=1, device_id=(dev, t), device_id_type=MESH)
+    pl.semaphore_signal(barrier, inc=1, device_id=(p, 1 - t), device_id_type=MESH)
+    pl.semaphore_wait(barrier, depth + 2)
+
+    sent = []
+
+    def go(copy):
+        copy.start()
+        sent.append(copy)
+        return copy
+
+    count = [0]
+
+    def gather_send(q, dev):
+        go(remote(block(a_all, q), block(a_all, q), ag_s.at[count[0]], ag_r.at[q], dev))
+        count[0] += 1
+
+    def gather_wait(q):
+        remote(block(a_all, q), block(a_all, q), ag_s.at[0], ag_r.at[q], core).wait_recv()
+
+    load_a.wait()
+    far = sorted(range(1, depth), key=lambda k: -min(k, depth - k))
+    gather_send(p, side)
+    for k in far:
+        gather_send(p, peer[k])
+    gather_send(p, core)
+
+    load_g.wait()
+    load_b.wait()
+    xs[0] = lax.dot_general(grad[...], b_mat[...], (((1,), (1,)), ((), ())), preferred_element_type=f32)
+    back = go(remote(xs.at[0], xr.at[0], x_s.at[0], x_r.at[0], p, 1 - t))
+
+    per_group = n // groups
+    group = p // per_group
+    offset = (p % per_group) * tokens
+    slots = (
+        lax.broadcasted_iota(jnp.int32, ratio_ref.shape, 0) * 128
+        + lax.broadcasted_iota(jnp.int32, ratio_ref.shape, 1)
+        + offset
+    )
+    live_total = jnp.int32(0)
+    live = jnp.zeros(ratio_ref.shape, f32)
+    token_adv = jnp.zeros(ratio_ref.shape, f32)
+    for g in range(groups):
+        here = jnp.full((1, 128), (group == g).astype(f32))
+        reward = [jnp.full((1, 128), rew_ref[g, i]).astype(f32) for i in range(rollouts)]
+        center = sum(reward) / rollouts
+        spread = sum((r - center) * (r - center) for r in reward) / rollouts
+        scale = jnp.sqrt(spread + 1.0)
+        end = jnp.int32(0)
+        for i in range(rollouts):
+            start = end
+            end = end + len_ref[g, i]
+            member = ((slots >= start) & (slots < end)).astype(f32) * here
+            live = live + member
+            token_adv = token_adv + member * ((reward[i] - center) / scale)
+        live_total = live_total + jnp.minimum(end, per_group * tokens)
+    ratio = jnp.exp(ratio_ref[...])
+    unclipped = ratio * token_adv
+    clipped = jnp.clip(ratio, 1.0 - clip_eps, 1.0 + clip_eps) * token_adv
+    token_loss = -jnp.minimum(unclipped, clipped)
+    slope = jnp.where(unclipped <= clipped, -unclipped, jnp.zeros_like(unclipped))
+    weight = live * slope
+    for i in range(tokens // 128):
+        coef[pl.ds(i * 128, 128), :] = jnp.broadcast_to(weight[i : i + 1, :], (128, 128)).T
+    factor = groups / jnp.full((1, 128), live_total).astype(f32)
+    loss_part = jnp.sum(jnp.sum(live * token_loss, axis=1, keepdims=True), axis=0, keepdims=True)
+
+    ls[0] = jnp.broadcast_to(loss_part, (8, 128))
+    first = go(remote(ls.at[0], l1, l_s.at[0], l_r.at[0], core))
+
+    back.wait_recv()
+    err[...] = (adapter_scale_factor * coef[...] * (xs[0] + xr[0])).astype(bf16)
+
+    load_x.wait()
+    tile = tile_of(ff, 1536)
+    steps = ff // tile
+
+    def partial_rows(i, _):
+        cols = pl.ds(pl.multiple_of(i * tile, 128), tile)
+        part[cols, :] = lax.dot_general(
+            act[:, cols], err[...], (((0,), (0,)), ((), ())), preferred_element_type=f32
+        ).astype(bf16)
+        return 0
+
+    near = [depth - k for k in far][::-1]
+    for j, k in enumerate(near):
+        lax.fori_loop(j * steps // len(near), (j + 1) * steps // len(near), partial_rows, 0)
+        q = peer[k]
+        gather_wait(q)
+        gather_send(q, side)
+        gather_send(q, core)
+
+    order = far + [0]
+    first_stage = {}
+    for yy in (1, 0):
+        for k in order:
+            yv = 1 - y if yy else y
+            i = k * 2 + yy
+            first_stage[k, yy] = go(
+                remote(block(part, at(zs[k], yv, 1 - c)), rs1.at[i], rs1_s.at[i], rs1_r.at[i], core)
+            )
+
+    first.wait_recv()
+    ls[1] = ls[0] + l1[...]
+    second = go(remote(ls.at[1], l2, l_s.at[1], l_r.at[1], side))
+
+    second_stage = {}
+    for k in order:
+        first_stage[k, 1].wait_recv()
+        own = block(part, at(zs[k], 1 - y, c))
+        own[...] = (own[...].astype(f32) + rs1[k * 2 + 1].astype(f32)).astype(bf16)
+        second_stage[k] = go(remote(own, rs2.at[k], rs2_s.at[k], rs2_r.at[k], side))
+
+    second.wait_recv()
+    lz[z] = ls[1] + l2[...]
+    third = [go(remote(lz.at[z], lz.at[z], lz_s.at[k], lz_r.at[k], peer[k])) for k in range(1, depth)]
+
+    for k in [0] + near:
+        q = at(zs[k], 1 - y, c)
+        gather_wait(q)
+        gather_send(q, core)
+    for k in range(depth):
+        gather_wait(at(zs[k], y, 1 - c))
+    for k in range(depth):
+        gather_wait(at(zs[k], 1 - y, 1 - c))
+
+    def low_rows(i, total):
+        cols = pl.ds(pl.multiple_of(i * tile, 128), tile)
+        return total + jnp.dot(act[:, cols], a_all[cols, :], preferred_element_type=f32)
+
+    xs[1] = lax.fori_loop(0, steps, low_rows, jnp.zeros((tokens, rank), f32))
+    low = go(remote(xs.at[1], xr.at[1], x_s.at[1], x_r.at[1], p, 1 - t))
+
+    third_stage = {}
+    for k in far:
+        first_stage[k, 0].wait_recv()
+        second_stage[k].wait_recv()
+        own = block(part, at(zs[k], y, c))
+        own[...] = (
+            own[...].astype(f32) + rs1[k * 2].astype(f32) + rs2[k].astype(f32)
+        ).astype(bf16)
+        third_stage[k] = go(remote(own, rs3.at[k], rs3_s.at[k], rs3_r.at[k], peer[k]))
+
+    low.wait_recv()
+    weighted = coef[...] * (xs[1] + xr[1])
+    high = weighted.astype(bf16)
+    rest = weighted - high.astype(f32)
+    middle = rest.astype(bf16)
+    last = (rest - middle.astype(f32)).astype(bf16)
+    width = grad.shape[1]
+    wide = tile_of(width, 640)
+    for i in range(width // wide):
+        cols = pl.ds(i * wide, wide)
+        g = grad[:, cols]
+        total = sum(
+            lax.dot_general(w, g, (((0,), (0,)), ((), ())), preferred_element_type=f32)
+            for w in (last, middle, high)
+        )
+        gb[:, cols] = total
+        gbs[:, cols] = total.astype(bf16)
+
+    half, quarter, chunk = rank // 2, rank // 4, width // depth
+    lane = pl.multiple_of(c * half, 16)
+    other = pl.multiple_of((1 - c) * half, 16)
+    one = go(remote(gbs.at[pl.ds(other, half)], gb1, g_s.at[0], g_r.at[0], core))
+    one.wait_recv()
+    away = pl.multiple_of((1 - y) * quarter, 16)
+    stay = pl.multiple_of(y * quarter, 16)
+    mine = pl.multiple_of(lane + stay, 16)
+    gb2s[...] = (
+        gb[pl.ds(pl.multiple_of(lane + away, 16), quarter), :] + gb1[pl.ds(away, quarter), :].astype(f32)
+    ).astype(bf16)
+    two = go(remote(gb2s, gb2, g_s.at[1], g_r.at[1], side))
+
+    first_stage[0, 0].wait_recv()
+    second_stage[0].wait_recv()
+    total = block(part, p)[...].astype(f32) + rs1[0].astype(f32) + rs2[0].astype(f32)
+    out_a[...] = total
+
+    two.wait_recv()
+    total = (
+        gb[pl.ds(mine, quarter), :]
+        + gb1[pl.ds(stay, quarter), :].astype(f32)
+        + gb2[...].astype(f32)
+    )
+    gb3s[...] = total.astype(bf16)
+    gb[pl.ds(mine, quarter), :] = total
+
+    def chunk_of(zz):
+        return pl.ds(pl.multiple_of(zz * chunk, 128), chunk)
+
+    three = {
+        k: go(remote(gb3s.at[:, chunk_of(zs[k])], gb3.at[k], gz_s.at[k], gz_r.at[k], peer[k]))
+        for k in far
+    }
+
+    for k in far:
+        third_stage[k].wait_recv()
+        out_a[...] = out_a[...] + rs3[k].astype(f32)
+    out_a[...] = factor * out_a[...]
+    for copy in third:
+        copy.wait_recv()
+    total = lz[0]
+    for i in range(1, depth):
+        total = total + lz[i]
+    out_loss[...] = factor * total
+
+    for k in far:
+        three[k].wait_recv()
+    total = gb[pl.ds(mine, quarter), chunk_of(z)]
+    for k in far:
+        total = total + gb3[k].astype(f32)
+    scaled = jnp.full((1, 128), adapter_scale_factor) * factor
+    fin[pl.ds(mine, quarter), chunk_of(z)] = (scaled[:, :1] * total).astype(bf16)
+
+    piece = fin.at[pl.ds(mine, quarter), chunk_of(z)]
+    four = {k: go(remote(piece, piece, fz_s.at[k], fz_r.at[k], peer[k])) for k in far}
+    for k in far:
+        four[k].wait_recv()
+    piece = fin.at[pl.ds(mine, quarter)]
+    five = go(remote(piece, piece, g_s.at[2], g_r.at[2], side))
+    five.wait_recv()
+    piece = fin.at[pl.ds(lane, half)]
+    six = go(remote(piece, piece, g_s.at[3], g_r.at[3], core))
+    six.wait_recv()
+    out_b[...] = fin[...].astype(f32)
+    for copy in sent:
+        copy.wait_send()
+
+
+def fused_local(activations, output_gradient, adapter_a, adapter_b, log_ratio, lengths, rewards):
+    n = lax.axis_size("dp")
+    depth = n // 4
+    tokens, ff = activations.shape
+    rows, rank = adapter_a.shape[1:]
+    width = output_gradient.shape[1]
+    dma = pltpu.SemaphoreType.DMA
+    vmem, anywhere = pl.BlockSpec(memory_space=pltpu.VMEM), pl.BlockSpec(memory_space=pl.ANY)
+    scalars = pl.BlockSpec(memory_space=pltpu.SMEM)
+    quarter, chunk = rank // 4, width // depth
+    grad_a, grad_b, loss = pl.pallas_call(
+        functools.partial(fused_kernel, n, lengths.shape[0], lengths.shape[1]),
+        out_shape=(
+            jax.ShapeDtypeStruct((rows, rank), f32),
+            jax.ShapeDtypeStruct((rank, width), f32),
+            jax.ShapeDtypeStruct((8, 128), f32),
+        ),
+        in_specs=[anywhere] * 4 + [vmem, scalars, scalars],
+        out_specs=(vmem, vmem, vmem),
+        scratch_shapes=[
+            pltpu.VMEM((tokens, ff), bf16),
+            pltpu.VMEM((tokens, width), bf16),
+            pltpu.VMEM((rank, width), bf16),
+            pltpu.VMEM((ff, rank), bf16),
+            pltpu.VMEM((ff, rank), bf16),
+            pltpu.VMEM((2 * depth, rows, rank), bf16),
+            pltpu.VMEM((depth, rows, rank), bf16),
+            pltpu.VMEM((depth, rows, rank), bf16),
+            pltpu.VMEM((2, tokens, rank), f32),
+            pltpu.VMEM((2, tokens, rank), f32),
+            pltpu.VMEM((tokens, rank), f32),
+            pltpu.VMEM((tokens, rank), bf16),
+            pltpu.VMEM((rank, width), f32),
+            pltpu.VMEM((rank, width), bf16),
+            pltpu.VMEM((rank // 2, width), bf16),
+            pltpu.VMEM((quarter, width), bf16),
+            pltpu.VMEM((quarter, width), bf16),
+            pltpu.VMEM((quarter, width), bf16),
+            pltpu.VMEM((depth, quarter, chunk), bf16),
+            pltpu.VMEM((rank, width), bf16),
+            pltpu.VMEM((2, 8, 128), f32),
+            pltpu.VMEM((8, 128), f32),
+            pltpu.VMEM((8, 128), f32),
+            pltpu.VMEM((depth, 8, 128), f32),
+            dma((4,)), dma((n - 1 + 0,)), dma((n,)),
+            dma((2 * depth,)), dma((2 * depth,)),
+            dma((depth,)), dma((depth,)), dma((depth,)), dma((depth,)),
+            dma((2,)), dma((2,)),
+            dma((4,)), dma((4,)), dma((depth,)), dma((depth,)), dma((depth,)), dma((depth,)),
+            dma((2,)), dma((2,)), dma((depth,)), dma((depth,)),
+        ],
+        compiler_params=pltpu.CompilerParams(
+            collective_id=0, has_side_effects=True, vmem_limit_bytes=48 * 1024 * 1024
+        ),
+        name="fused",
+    )(
+        activations, output_gradient, adapter_a[0], adapter_b,
+        log_ratio.reshape(-1, 128), lengths, rewards,
+    )
+    return grad_a[None], grad_b, loss[0, 0]
+
+
+def fits(mesh):
+    n, split = mesh.shape["dp"], mesh.shape["tensor"]
+    return n % 4 == 0 and 4 <= n <= 16 and split == 2
+
+
+def local(activations, output_gradient, adapter_a, adapter_b, log_ratio, lengths, rewards):
+    n = lax.axis_size("dp")
+    rows, rank = adapter_a.shape[1:]
+    width, ff = output_gradient.shape[1], activations.shape[1]
+    small = 2 * activations.size + 8 * ff * rank < 32 * 1024 * 1024
+    aligned = (
+        rows % 16 == 0
+        and rank == 128
+        and activations.shape[0] % 128 == 0
+        and ff % 128 == 0
+        and width % (128 * (n // 4)) == 0
+        and n % lengths.shape[0] == 0
+    )
+    run = fused_local if small and aligned else plain_local
+    return run(activations, output_gradient, adapter_a, adapter_b, log_ratio, lengths, rewards)
+
+
 def solution(mesh):
     in_specs = (
         P("dp", "tensor"),
@@ -87,4 +458,5 @@
         P(),
     )
     out_specs = (P("tensor", "dp", None), P(None, "tensor"), P())
-    return jax.shard_map(local, mesh=mesh, in_specs=in_specs, out_specs=out_specs, check_vma=False)
+    body = local if fits(mesh) else plain_local
+    return jax.shard_map(body, mesh=mesh, in_specs=in_specs, out_specs=out_specs, check_vma=False)

time: 291 us -> 88.3 us (0.30)
  waiting for transfers between devices: 200 us -> 0 us
  Pallas kernels: 0 us -> 79.7 us
  blocking collectives: 33.6 us -> 0 us
  matrix products: 18.8 us -> 0 us
  between operations: 17.6 us -> 0.66 us
  other arithmetic: 7.82 us -> 0 us
  local copies, waits for them, and re-layouts: 12.2 us -> 7.65 us
    unnamed x5 -> x0, waiting for transfers between devices: 91.8 us -> none
    pallas_call x0 -> x1, Pallas kernels: none -> 79.7 us  [fused_local(): pl.pallas_call(functools.partial(fused_kernel, n, lengths.shape[0], lengt...]
    psum x2 -> x0, waiting for transfers between devices: 64.7 us -> none  [the longest x1 44 us: local(): lax.psum((local_adapter_b_gradient, loss_local, live_count), 'dp')]
    all_gather x1 -> x0, waiting for transfers between devices: 43.8 us -> none  [local(): lax.all_gather(adapter_a, 'dp', axis=1, tiled=True)[0]]
    psum x1 -> x0, blocking collectives: 33.6 us -> none  [local(): lax.psum((local_adapter_b_gradient, loss_local, live_count), 'dp')]
    dot_general x4 -> x0, matrix products: 18.8 us -> none  [the longest x1 7.15 us: local(): lax.dot_general(columns, error_rows, (((0,), (0,)), ((), ())), preferred_...]
    unnamed x9 -> x14, local copies, waits for them, and re-layouts: 11.4 us -> 7.14 us
    reduce_sum x3 -> x0, other arithmetic: 3.21 us -> none  [the longest x1 1.26 us: token_terms(): spread = jnp.mean((reward - center) * (reward - center))]
  transfers between devices with their start and end apart: 4 -> 0, of which waited for: 4 -> 0; matrix products, arithmetic and copies ran while one was open for 9% -> 0% of each run, Pallas kernels for 0% -> 0%
where the time goes in v1:
time: 88.3 us; the launch traced here: 88 us
  Pallas kernels  79.7 us (90%)
  local copies, waits for them, and re-layouts  7.65 us (9%)
    pallas_call x1, Pallas kernels, fused_local(): pl.pallas_call(functools.partial(fused_kernel, n, lengths.shape[0], lengt...  79.7 us
    unnamed x14, local copies, waits for them, and re-layouts  7.14 us

profile of v1, /device:TPU:0, one launch (start us, length us, event | category | flops | bytes accessed | tf_op | source)
XLA Modules:
  0.0 88.0 jit_solution(2955415881586334181)
XLA Ops:
  0.6 0.0 copy-start
  0.6 1.3 %copy-done = bf16[256,2560]{1,0:T(8,128)(2,1)S(1)} copy-done((bf16[256,2560]{1,0:T(8,128)(2,1)S(1)}, bf16[256,2560]{1,0:T(8,128)(2,1)}, u32[]{:S(2)}) %copy-start) | copy-done | bytes 1310744
  1.9 0.0 copy-start.1
  2.0 1.1 %copy-done.1 = bf16[128,2560]{1,0:T(8,128)(2,1)S(1)} copy-done((bf16[128,2560]{1,0:T(8,128)(2,1)S(1)}, bf16[128,2560]{1,0:T(8,128)(2,1)}, u32[]{:S(2)}) %copy-start.1) | copy-done | bytes 655384
  3.0 0.0 copy-start.2
  3.0 0.9 %copy-done.2 = bf16[1,864,128]{2,1,0:T(8,128)(2,1)S(1)} copy-done((bf16[1,864,128]{2,1,0:T(8,128)(2,1)S(1)}, bf16[1,864,128]{2,1,0:T(8,128)(2,1)}, u32[]{:S(2)}) %copy-start.2) | copy-done | bytes 221208
  4.0 0.0 copy-start.3
  4.0 0.7 copy-done.3
  4.7 0.0 copy-start.4
  4.7 0.7 copy-done.4
  5.3 0.0 copy-start.5
  5.3 0.7 copy-done.5
  6.0 79.7 %fused.1 = (f32[864,128]{1,0:T(8,128)S(1)}, f32[128,2560]{1,0:T(8,128)S(1)}, f32[8,128]{1,0:T(8,128)S(1)}) custom-call(bf16[256,13824]{1,0:T(8,128)(2,1)} %act_hbm.1, bf16[256,2560]{1,0:T(8,128)(2,1)S(1)} %copy-done, bf16[864,128]{1,0:T(8,128)(2,1)S(1)} %bitcast.5, bf16[128,2560]{1,0:T(8,128)(2,1)S(1)} %copy-done.1, f32[2,128]{1,0:T(2,128)S(1)} %bitcast.6, ...), custom_call_target="tpu_custom_call" | custom-call | tf_op jit(solution)/shard_map/fused/pallas_call | solution.py:376
  85.6 0.5 slice.3
  86.1 0.8 copy.12
  86.9 1.1 %copy.13 = f32[128,2560]{1,0:T(8,128)} copy(f32[128,2560]{1,0:T(8,128)S(1)} %get-tuple-element.13) | data formatting | bytes 2621440
Async XLA Ops:
  0.6 1.3 %copy-start = (bf16[256,2560]{1,0:T(8,128)(2,1)S(1)}, bf16[256,2560]{1,0:T(8,128)(2,1)}, u32[]{:S(2)}) copy-start(bf16[256,2560]{1,0:T(8,128)(2,1)} %grad_hbm.1) | copy-start | bytes 3932164
  1.9 1.1 %copy-start.1 = (bf16[128,2560]{1,0:T(8,128)(2,1)S(1)}, bf16[128,2560]{1,0:T(8,128)(2,1)}, u32[]{:S(2)}) copy-start(bf16[128,2560]{1,0:T(8,128)(2,1)} %b_hbm.1) | copy-start | bytes 1966084
  3.0 0.9 %copy-start.2 = (bf16[1,864,128]{2,1,0:T(8,128)(2,1)S(1)}, bf16[1,864,128]{2,1,0:T(8,128)(2,1)}, u32[]{:S(2)}) copy-start(bf16[1,864,128]{2,1,0:T(8,128)(2,1)} %param.9) | copy-start | bytes 663556
  4.0 0.7 copy-start.3
  4.7 0.7 copy-start.4
  5.3 0.7 copy-start.5
